TPU v7x, 32 devices: a whole 2x2x4 slice. The times are simulated.
32 devices in a mesh: section: 4 (over y, x), dp: 8 (over z, core).
Axes of the slice: x: 2, y: 2, z: 4, core: 2. Of those that a mesh axis runs over, the one named last changes fastest.
Arguments:
- block_inputs: bfloat16 [4, 4, 512, 2048], P('section', None, 'dp'), may hold values from -6 to 6
- mixed_inputs: bfloat16 [4, 4, 512, 2048], P('section', None, 'dp'), may hold values from -6 to 6
- token_ids: int32 [4, 512], P(None, 'dp'), may hold values from 0 to 2047
- target_ids: int32 [4, 512], P(None, 'dp'), may hold values from 0 to 2047
- final_gain: float32 [2048], replicated, may hold values from 0.5 to 1.5
- out_weight: bfloat16 [4, 2048, 2048], P('section'), may hold values from -0.0625 to 0.0625
- head_weight: bfloat16 [2048, 2048], P('section'), may hold values from -0.375 to 0.375
- out_master: float32 [4, 2048, 2048], P('section', 'dp'), may hold values from -0.125 to 0.125
- out_first: float32 [4, 2048, 2048], P('section', 'dp'), may hold values from -1.25 to 1.25
- out_second: float32 [4, 2048, 2048], P('section', 'dp'), may hold values from 1 to 20
- head_master: float32 [2048, 2048], P(('section', 'dp')), may hold values from -0.125 to 0.125
- head_first: float32 [2048, 2048], P(('section', 'dp')), may hold values from -0.75 to 0.75
- head_second: float32 [2048, 2048], P(('section', 'dp')), may hold values from 0.3 to 6
- embed_master: float32 [2048, 2048], P(('section', 'dp')), may hold values from -0.125 to 0.125
- embed_first: float32 [2048, 2048], P(('section', 'dp')), may hold values from -0.0625 to 0.0625
- embed_second: float32 [2048, 2048], P(('section', 'dp')), may hold values from 0.0024414062 to 0.048828125
Outputs:
- out_master_next: float32 [4, 2048, 2048], P('section', 'dp')
- out_first_next: float32 [4, 2048, 2048], P('section', 'dp')
- out_second_next: float32 [4, 2048, 2048], P('section', 'dp')
- head_master_next: float32 [2048, 2048], P(('section', 'dp'))
- head_first_next: float32 [2048, 2048], P(('section', 'dp'))
- head_second_next: float32 [2048, 2048], P(('section', 'dp'))
- embed_master_next: float32 [2048, 2048], P(('section', 'dp'))
- embed_first_next: float32 [2048, 2048], P(('section', 'dp'))
- embed_second_next: float32 [2048, 2048], P(('section', 'dp'))
Inputs may be any that keep to these rules, and one draw needn't show every extreme that they name: `token_ids`: every token id lies in 0 to 2047. `target_ids`: every target id lies in 0 to 2047.
All inputs are finite; a program needn't handle non-finite values.
Results may differ from a plain program's by a relative error of at most 0.00155.
Values may be sent and summed in bfloat16 or wider, within the bound.
A program may use at most 128 MiB of HBM per device.

v0:
```python
import jax
import jax.numpy as jnp
from jax import lax
from jax.sharding import PartitionSpec as P

norm_eps = 1e-05
beta_first = 0.9
beta_second = 0.95
adam_eps = 1e-05
learning_rate = 0.0003
decay_rate = 0.1


def broadcast(value, axis, source):
    kept = jnp.where(lax.axis_index(axis) == source, value, 0).astype(value.dtype)
    return lax.psum(kept, axis)


def combined_all(part, axis, combine):
    gathered = jax.tree.map(lambda a: lax.all_gather(a, axis), part)

    def take(source):
        return jax.tree.map(lambda a: lax.dynamic_index_in_dim(a, source, 0, False), gathered)

    return lax.fori_loop(
        1, lax.axis_size(axis), lambda source, state: combine(state, take(source)), take(0)
    )


def from_behind(block, axis, distance):
    devices = range(lax.axis_size(axis))
    route = [(i - distance, i) for i in devices if i - distance in devices]
    return lax.ppermute(block, axis, route)


def times_transposed(former, latter):
    return lax.dot_general(
        former, latter, (((1,), (1,)), ((), ())), preferred_element_type=jnp.float32
    )


def transposed_times(former, latter):
    return lax.dot_general(
        former, latter, (((0,), (0,)), ((), ())), preferred_element_type=jnp.float32
    )


def plain_times(former, latter):
    return jnp.dot(former, latter, preferred_element_type=jnp.float32)


def normalize(values, gain):
    inverse = lax.rsqrt(jnp.mean(values * values, axis=-1, keepdims=True) + norm_eps)
    return (inverse, values * inverse * gain)


def norm_backward(values, inverse, scaled_cotangent):
    unit = values * inverse
    return inverse * (
        scaled_cotangent - unit * jnp.mean(scaled_cotangent * unit, axis=-1, keepdims=True)
    )


def adam_update(master, first, second, gradient):
    first_next = beta_first * first + (1.0 - beta_first) * gradient
    second_next = beta_second * second + (1.0 - beta_second) * gradient * gradient
    master_next = master - learning_rate * (
        first_next / (jnp.sqrt(second_next) + adam_eps) + decay_rate * master
    )
    return (master_next, first_next, second_next)


def join_rows(former, latter):
    top = jnp.maximum(former[0], latter[0])
    return (top, former[1] * jnp.exp(former[0] - top) + latter[1] * jnp.exp(latter[0] - top))


def local(
    block_inputs,
    mixed_inputs,
    token_ids,
    target_ids,
    final_gain,
    out_weight,
    head_weight,
    out_master,
    out_first,
    out_second,
    head_master,
    head_first,
    head_second,
    embed_master,
    embed_first,
    embed_second,
):
    sections = lax.axis_size("section")
    section = lax.axis_index("section")
    last = sections - 1
    batches, rows, width = mixed_inputs[0].shape
    flat_mixed = mixed_inputs[0].reshape(batches * rows, width)
    wide = block_inputs[0].reshape(batches * rows, width).astype(jnp.float32)
    slice_rows = head_weight.shape[0]
    vocabulary_start = section * slice_rows
    columns = vocabulary_start + lax.broadcasted_iota(jnp.int32, (1, slice_rows), 1)
    final = wide + times_transposed(flat_mixed, out_weight[0])
    final_inverse, final_scaled = normalize(final, final_gain)
    shared_hidden = broadcast(final_scaled.astype(jnp.bfloat16), "section", last)
    logits = times_transposed(shared_hidden, head_weight)
    local_top = jnp.max(logits, axis=1)
    local_weights = jnp.exp(logits - local_top[:, None])
    row_top, row_total = combined_all(
        (local_top, jnp.sum(local_weights, axis=1)), "section", join_rows
    )
    predicted = local_weights * (jnp.exp(local_top - row_top) / row_total)[:, None]
    target_flat = target_ids.reshape(-1)
    logit_cotangent = jnp.where(target_flat[:, None] == columns, predicted - 1.0, predicted).astype(
        jnp.bfloat16
    )
    hidden_cotangent = lax.psum(plain_times(logit_cotangent, head_weight), "section")
    top_cotangent = norm_backward(final, final_inverse, hidden_cotangent * final_gain).astype(
        jnp.bfloat16
    )

    def reduce_head():

        def head_term(count):
            part = lax.slice_in_dim(logit_cotangent, 0, count, axis=1)
            return transposed_times(part, shared_hidden)

        return lax.psum_scatter(
            head_term(head_master.shape[0] * lax.axis_size("dp")),
            "dp",
            scatter_dimension=0,
            tiled=True,
        )

    def relay(step, held):
        received = from_behind(held, "section", -1)
        return jnp.where(section == last, held, received)

    cotangent = lax.fori_loop(0, last, relay, top_cotangent)
    out_term = transposed_times(cotangent, flat_mixed)
    out_gradient = lax.psum_scatter(out_term, "dp", scatter_dimension=0, tiled=True)
    tokens_flat = token_ids.reshape(-1)

    def embed_term(count):
        wanted = vocabulary_start + lax.broadcasted_iota(jnp.int32, (1, count), 1)
        marks = (tokens_flat[:, None] == wanted).astype(jnp.bfloat16)
        return transposed_times(marks, cotangent)

    embed_gradient = lax.psum_scatter(
        embed_term(embed_master.shape[0] * lax.axis_size("dp")),
        "dp",
        scatter_dimension=0,
        tiled=True,
    )
    head_gradient = reduce_head()
    out_out = adam_update(out_master, out_first, out_second, out_gradient.reshape(out_master.shape))
    head_out = adam_update(head_master, head_first, head_second, head_gradient)
    embed_out = adam_update(embed_master, embed_first, embed_second, embed_gradient)
    return (
        out_out[0],
        out_out[1],
        out_out[2],
        head_out[0],
        head_out[1],
        head_out[2],
        embed_out[0],
        embed_out[1],
        embed_out[2],
    )


def solution(mesh):
    return jax.shard_map(
        local,
        mesh=mesh,
        in_specs=(
            P("section", None, "dp", None),
            P("section", None, "dp", None),
            P(None, "dp"),
            P(None, "dp"),
            P(),
            P("section", None, None),
            P("section", None),
            P("section", "dp", None),
            P("section", "dp", None),
            P("section", "dp", None),
            P(("section", "dp"), None),
            P(("section", "dp"), None),
            P(("section", "dp"), None),
            P(("section", "dp"), None),
            P(("section", "dp"), None),
            P(("section", "dp"), None),
        ),
        out_specs=(
            P("section", "dp", None),
            P("section", "dp", None),
            P("section", "dp", None),
            P(("section", "dp"), None),
            P(("section", "dp"), None),
            P(("section", "dp"), None),
            P(("section", "dp"), None),
            P(("section", "dp"), None),
            P(("section", "dp"), None),
        ),
        check_vma=False,
    )
```

profile of v0, /device:TPU:0, one launch (start us, length us, event | category | flops | bytes accessed | tf_op | source)
XLA Modules:
  0.0 481.8 jit_solution(1719331455801563350)
XLA Ops:
  7.3 7.8 %multiply_reduce_fusion.1 = (f32[256]{0:T(256)S(1)}, f32[256,2048]{1,0:T(8,128)}) fusion(bf16[256,2048]{1,0:T(8,128)(2,1)} %bitcast.42, bf16[1,2048,2048]{2,1,0:T(8,128)(2,1)} %param.25, bf16[256,2048]{1,0:T(8,128)(2,1)} %bitcast.52), kind=kOutput, calls=%fused_computation.15 | convolution fusion | flops 2149580544 | bytes 12583936 | tf_op jit(solution)/shard_map/dot_general | solution.py:37
  15.1 2.9 fusion.7
  18.1 54.9 %all-reduce.3.cloned.1.call-done = bf16[256,2048]{1,0:T(8,128)(2,1)} async-done(((bf16[256,2048]{1,0:T(8,128)(2,1)}), bf16[256,2048]{1,0:T(8,128)(2,1)}) %all-reduce.3.cloned.1.call-update) | async-done | bytes 1048592 | tf_op jit(solution)/shard_map/psum | solution.py:16
  73.0 2.0 fusion.23
  75.3 7.9 %all-gather.3 = f32[4,1,256]{2,1,0:T(1,128)S(1)} all-gather(f32[1,1,256]{2,1,0:T(1,128)S(1)} %bitcast.51), channel_id=3, replica_groups=mesh['section'=4,'dp'=8] {'section'}, dimensions={0}, use_global_device_ids=true | all-gather | bytes 5120 | tf_op jit(solution)/shard_map/all_gather | solution.py:20
  83.3 7.0 %all-gather.2 = f32[4,1,256]{2,1,0:T(1,128)S(1)} all-gather(f32[1,1,256]{2,1,0:T(1,128)S(1)} %bitcast.46), channel_id=2, replica_groups=mesh['section'=4,'dp'=8] {'section'}, dimensions={0}, use_global_device_ids=true | all-gather | bytes 5120 | tf_op jit(solution)/shard_map/all_gather | solution.py:20
  90.5 2.1 fusion.18
  93.8 2.9 fusion.16
  97.5 64.4 %all-reduce.5.cloned.1.call-done = f32[256,2048]{1,0:T(8,128)} async-done(((f32[256,2048]{1,0:T(8,128)}), f32[256,2048]{1,0:T(8,128)}) %all-reduce.5.cloned.1.call-update) | async-done | bytes 2097168 | tf_op jit(solution)/shard_map/psum | solution.py:119
  161.9 2.1 multiply_reduce_fusion
  165.2 79.4 %while.30 = (s32[]{:T(128)}, bf16[256,2048]{1,0:T(8,128)(2,1)S(1)}, pred[]{:T(512)}, s32[]{:T(128)}) while((s32[]{:T(128)}, bf16[256,2048]{1,0:T(8,128)(2,1)S(1)}, pred[]{:T(512)}, s32[]{:T(128)}) %tuple.77), condition=%wide.region_9.10_spmd, body=%wide.region_8.9_spmd.sunk | while | flops 524290 | bytes 7340126 | solution.py:141
  165.2 1.3 collective-permute-start
  166.5 25.2 %collective-permute-done = bf16[256,2048]{1,0:T(8,128)(2,1)S(1)} collective-permute-done((bf16[256,2048]{1,0:T(8,128)(2,1)S(1)}, bf16[256,2048]{1,0:T(8,128)(2,1)S(1)}, u32[]{:S(2)}, u32[]{:S(2)}) %collective-permute-start) | collective-permute-done | bytes 1048608 | tf_op jit(solution)/shard_map/while/body/eval_jaxpr/ppermute | solution.py:33
  192.0 1.3 collective-permute-start
  193.3 25.1 %collective-permute-done = bf16[256,2048]{1,0:T(8,128)(2,1)S(1)} collective-permute-done((bf16[256,2048]{1,0:T(8,128)(2,1)S(1)}, bf16[256,2048]{1,0:T(8,128)(2,1)S(1)}, u32[]{:S(2)}, u32[]{:S(2)}) %collective-permute-start) | collective-permute-done | bytes 1048608 | tf_op jit(solution)/shard_map/while/body/eval_jaxpr/ppermute | solution.py:33
  218.8 1.3 collective-permute-start
  220.1 24.3 %collective-permute-done = bf16[256,2048]{1,0:T(8,128)(2,1)S(1)} collective-permute-done((bf16[256,2048]{1,0:T(8,128)(2,1)S(1)}, bf16[256,2048]{1,0:T(8,128)(2,1)S(1)}, u32[]{:S(2)}, u32[]{:S(2)}) %collective-permute-start) | collective-permute-done | bytes 1048608 | tf_op jit(solution)/shard_map/while/body/eval_jaxpr/ppermute | solution.py:33
  244.7 2.8 fusion.11
  248.7 8.1 %fusion.24 = f32[2048,2048]{1,0:T(8,128)} fusion(bf16[256,2048]{1,0:T(8,128)(2,1)S(1)} %get-tuple-element.183, bf16[256,2048]{1,0:T(8,128)(2,1)S(1)} %bitcast.43), kind=kOutput, calls=%fused_computation.42 | convolution fusion | flops 2147483648 | bytes 18874368 | tf_op jit(solution)/shard_map/dot_general | solution.py:43
  258.2 2.4 multiply_subtract_fusion.2
  260.5 38.1 %reduce-scatter.8.cloned.1.call-done = f32[64,2048]{1,0:T(8,128)} async-done(((f32[512,2048]{1,0:T(8,128)}), f32[64,2048]{1,0:T(8,128)}) %reduce-scatter.8.cloned.1.call-update) | async-done | bytes 524304 | tf_op jit(solution)/shard_map/reduce_scatter | solution.py:151
  298.6 2.4 multiply_subtract_fusion.1
  301.0 166.7 %reduce-scatter.4.cloned.1.call-done = f32[256,2048]{1,0:T(8,128)} async-done(((f32[2048,2048]{1,0:T(8,128)}), f32[256,2048]{1,0:T(8,128)}) %reduce-scatter.4.cloned.1.call-update) | async-done | bytes 2097168 | tf_op jit(solution)/shard_map/reduce_scatter | solution.py:143
  467.7 7.6 %multiply_subtract_fusion = (f32[1,256,2048]{2,1,0:T(8,128)}, f32[1,256,2048]{2,1,0:T(8,128)}, f32[1,256,2048]{2,1,0:T(8,128)}) fusion(f32[1,256,2048]{2,1,0:T(8,128)} %param.27, f32[256,2048]{1,0:T(8,128)} %reduce-scatter.4.cloned.1.call-done, f32[1,256,2048]{2,1,0:T(8,128)} %param.29, f32[1,256,2048]{2,1,0:T(8,128)} %param.28), kind=kLoop, calls=%fused_computation.11 | loop fusion | flops 6815744 | bytes 14680064 | tf_op jit(solution)/shard_map/sub | solution.py:67
  (65 shorter events, 7.2 us)
Async XLA Ops:
  7.2 65.9 %copy-start = (bf16[512,2048]{1,0:T(8,128)(2,1)S(1)}, bf16[512,2048]{1,0:T(8,128)(2,1)}, u32[]{:S(2)}) copy-start(bf16[512,2048]{1,0:T(8,128)(2,1)} %param.26) | copy-start | bytes 6291460
  7.2 65.8 %all-reduce.3.cloned.1.call-start = ((), (), s32[]{:S(2)}) async-start(), calls=%async_computation.3 | async-start | bytes 2097152 | tf_op jit(solution)/shard_map/psum | solution.py:16
  7.2 7.8 %copy-start.13 = (f32[2048]{0:T(1024)S(1)}, f32[2048]{0:T(1024)}, u32[]{:S(2)}) copy-start(f32[2048]{0:T(1024)} %param.24) | copy-start | bytes 24580
  15.1 3.0 copy-start.14
  18.0 143.9 %all-reduce.5.cloned.1.call-start = ((), (), s32[]{:S(2)}) async-start(), calls=%async_computation.4 | async-start | bytes 4194304 | tf_op jit(solution)/shard_map/psum | solution.py:119
  92.6 1.2 copy-start.6
  92.6 164.2 %reduce-scatter.6.cloned.1.call-start = ((), (), s32[]{:S(2)}) async-start(), calls=%async_computation.6 | async-start | bytes 4718592 | tf_op jit(solution)/shard_map/reduce_scatter | solution.py:130
  96.7 0.7 copy-start.15
  96.7 65.1 %copy-start.2 = (f32[256,2048]{1,0:T(8,128)S(1)}, f32[256,2048]{1,0:T(8,128)}, u32[]{:S(2)}) copy-start(f32[256,2048]{1,0:T(8,128)} %get-tuple-element.214) | copy-start | bytes 6291460
  96.7 201.9 %reduce-scatter.8.cloned.1.call-start = ((), (), s32[]{:S(2)}) async-start(), calls=%async_computation.7 | async-start | bytes 4718592 | tf_op jit(solution)/shard_map/reduce_scatter | solution.py:151
  161.9 2.2 copy-start.3
  161.9 2.9 copy-start.4
  165.2 26.5 %collective-permute-start = (bf16[256,2048]{1,0:T(8,128)(2,1)S(1)}, bf16[256,2048]{1,0:T(8,128)(2,1)S(1)}, u32[]{:S(2)}, u32[]{:S(2)}) collective-permute-start(bf16[256,2048]{1,0:T(8,128)(2,1)S(1)} %get-tuple-element.304), channel_id=1, source_target_pairs={{8,0},{16,8},{24,16},{9,1},{17,9},{25,17},{10,2},{18,10},{26,18},{... | collective-permute-start | bytes 3145736 | tf_op jit(solution)/shard_map/while/body/eval_jaxpr/ppermute | solution.py:33
  192.0 26.4 %collective-permute-start = (bf16[256,2048]{1,0:T(8,128)(2,1)S(1)}, bf16[256,2048]{1,0:T(8,128)(2,1)S(1)}, u32[]{:S(2)}, u32[]{:S(2)}) collective-permute-start(bf16[256,2048]{1,0:T(8,128)(2,1)S(1)} %get-tuple-element.304), channel_id=1, source_target_pairs={{8,0},{16,8},{24,16},{9,1},{17,9},{25,17},{10,2},{18,10},{26,18},{... | collective-permute-start | bytes 3145736 | tf_op jit(solution)/shard_map/while/body/eval_jaxpr/ppermute | solution.py:33
  218.8 25.6 %collective-permute-start = (bf16[256,2048]{1,0:T(8,128)(2,1)S(1)}, bf16[256,2048]{1,0:T(8,128)(2,1)S(1)}, u32[]{:S(2)}, u32[]{:S(2)}) collective-permute-start(bf16[256,2048]{1,0:T(8,128)(2,1)S(1)} %get-tuple-element.304), channel_id=1, source_target_pairs={{8,0},{16,8},{24,16},{9,1},{17,9},{25,17},{10,2},{18,10},{26,18},{... | collective-permute-start | bytes 3145736 | tf_op jit(solution)/shard_map/while/body/eval_jaxpr/ppermute | solution.py:33
  247.4 1.2 copy-start.5
  247.5 220.3 %reduce-scatter.4.cloned.1.call-start = ((), (), s32[]{:S(2)}) async-start(), calls=%async_computation.5 | async-start | bytes 18874368 | tf_op jit(solution)/shard_map/reduce_scatter | solution.py:143
  256.8 1.0 copy-start.7
  256.8 1.2 copy-start.8
  256.8 1.4 copy-start.9
  256.8 41.8 %copy-start.10 = (f32[64,2048]{1,0:T(8,128)S(1)}, f32[64,2048]{1,0:T(8,128)}, u32[]{:S(2)}) copy-start(f32[64,2048]{1,0:T(8,128)} %param.33) | copy-start | bytes 1572868
  256.8 41.8 %copy-start.11 = (f32[64,2048]{1,0:T(8,128)S(1)}, f32[64,2048]{1,0:T(8,128)}, u32[]{:S(2)}) copy-start(f32[64,2048]{1,0:T(8,128)} %param.35) | copy-start | bytes 1572868
  256.9 41.8 %copy-start.12 = (f32[64,2048]{1,0:T(8,128)S(1)}, f32[64,2048]{1,0:T(8,128)}, u32[]{:S(2)}) copy-start(f32[64,2048]{1,0:T(8,128)} %param.34) | copy-start | bytes 1572868
  467.7 7.6 %copy-start.1 = (bf16[512,2048]{1,0:T(8,128)(2,1)S(1)}, bf16[512,2048]{1,0:T(8,128)(2,1)}, u32[]{:S(2)}) copy-start(bf16[512,2048]{1,0:T(8,128)(2,1)} %param.26) | copy-start | bytes 6291460
Sparse Core Ops, SparseCore 0:
  18.1 54.9 all-reduce.2
  92.8 69.0 all-reduce.4
  164.2 49.7 reduce-scatter.5
  247.6 50.9 reduce-scatter.7
  300.8 166.8 reduce-scatter.3
where the time goes:
time: 482 us
  waiting for transfers between devices  399 us (83%)
  matrix products  25.8 us (5%)
  other arithmetic  19 us (4%)
  blocking collectives  15 us (3%)
  between operations  13.9 us (3%)
  local copies, waits for them, and re-layouts  4.93 us (1%)
    reduce_scatter x1, waiting for transfers between devices, local(): lax.psum_scatter(out_term, 'dp', scatter_dimension=0, tiled=True)  167 us
    ppermute x3, waiting for transfers between devices, from_behind(): return lax.ppermute(block, axis, route)  74.7 us
    psum x1, waiting for transfers between devices, local(): lax.psum(plain_times(logit_cotangent, head_weight), 'section')  64.4 us
    psum x1, waiting for transfers between devices, broadcast(): return lax.psum(kept, axis)  54.9 us
    reduce_scatter x1, waiting for transfers between devices, local(): lax.psum_scatter(embed_term(embed_master.shape[0] * lax.axis_size('dp')),...  38.1 us
    all_gather x2, blocking collectives, combined_all(): gathered = jax.tree.map(lambda a: lax.all_gather(a, axis), part)  15 us
    dot_general x3, matrix products, transposed_times(): lax.dot_general(former, latter, (((0,), (0,)), ((), ())), preferred_eleme...  13.8 us
    sub x3, other arithmetic, adam_update(): master - learning_rate * (first_next / (jnp.sqrt(second_next) + adam_eps)...  12.3 us
  transfers between devices with their start and end apart: 8, of which 7 were waited for; matrix products, arithmetic and copies ran while one was open for 5% of the time, Pallas kernels for 0%

commit v1 on v0

v1 whole, which is shorter than its diff:
```python
import functools
import jax
import jax.numpy as jnp
from jax import lax
from jax.experimental import pallas as pl
from jax.experimental.pallas import tpu as pltpu
from jax.sharding import PartitionSpec as P

norm_eps = 1e-05
beta_first = 0.9
beta_second = 0.95
adam_eps = 1e-05
learning_rate = 0.0003
decay_rate = 0.1

MESH = pl.DeviceIdType.MESH


def times_transposed(former, latter):
    return lax.dot_general(
        former, latter, (((1,), (1,)), ((), ())), preferred_element_type=jnp.float32
    )


def transposed_times(former, latter):
    return lax.dot_general(
        former, latter, (((0,), (0,)), ((), ())), preferred_element_type=jnp.float32
    )


def plain_times(former, latter):
    return jnp.dot(former, latter, preferred_element_type=jnp.float32)


def adam_update(master, first, second, gradient):
    first_next = beta_first * first + (1.0 - beta_first) * gradient
    second_next = beta_second * second + (1.0 - beta_second) * gradient * gradient
    master_next = master - learning_rate * (
        first_next / (jnp.sqrt(second_next) + adam_eps) + decay_rate * master
    )
    return (master_next, first_next, second_next)


def greet(axis, size, me):
    barrier = pltpu.get_barrier_semaphore()
    for step in range(1, size):
        partner = lax.rem(me + step, size)
        pl.semaphore_signal(barrier, inc=1, device_id={axis: partner}, device_id_type=MESH)
    pl.semaphore_wait(barrier, size - 1)


def exchange_kernel(axis, size, modes, *refs):
    count = len(modes)
    ins, outs = refs[:count], refs[count : 2 * count]
    send_sem, recv_sem = refs[2 * count :]
    me = lax.axis_index(axis)
    greet(axis, size, me)
    copies = []
    for step in range(1, size):
        partner = lax.rem(me + step, size)
        for k, mode in enumerate(modes):
            copy = pltpu.make_async_remote_copy(
                src_ref=ins[k] if mode == "share" else ins[k].at[partner],
                dst_ref=outs[k].at[step - 1 if mode == "others" else me],
                send_sem=send_sem.at[k, step - 1],
                recv_sem=recv_sem.at[k, step - 1],
                device_id={axis: partner},
                device_id_type=MESH,
            )
            copy.start()
            copies.append(copy)
    for k, mode in enumerate(modes):
        if mode != "others":
            outs[k][me] = ins[k][me] if mode == "swap" else ins[k][...]
    for copy in copies:
        copy.wait()


def exchange(arrays, modes, axis, collective_id):
    size = lax.axis_size(axis)
    lead = {"swap": (size,), "share": (size,), "others": (size - 1,)}
    shapes = [
        jax.ShapeDtypeStruct(lead[mode] + (a.shape if mode == "share" else a.shape[1:]), a.dtype)
        for a, mode in zip(arrays, modes)
    ]
    return pl.pallas_call(
        functools.partial(exchange_kernel, axis, size, tuple(modes)),
        out_shape=shapes,
        in_specs=[pl.BlockSpec(memory_space=pltpu.VMEM)] * len(arrays),
        out_specs=[pl.BlockSpec(memory_space=pltpu.VMEM)] * len(arrays),
        scratch_shapes=[
            pltpu.SemaphoreType.DMA((len(arrays), size - 1)),
            pltpu.SemaphoreType.DMA((len(arrays), size - 1)),
        ],
        compiler_params=pltpu.CompilerParams(collective_id=collective_id, has_side_effects=True),
    )(*arrays)


def spread_kernel(axis, size, chunks, in_ref, out_ref, send_sem, recv_sem):
    me = lax.axis_index(axis)
    place = me
    shift = me // 2
    while_size = size
    while while_size > 2:
        place = place ^ shift
        shift = shift // 2
        while_size //= 2

    def device_at(position):
        position = lax.rem(position + size, size)
        return position ^ (position // 2)

    source_place = 0
    for candidate in range(size):
        if candidate ^ (candidate // 2) == size - 1:
            source_place = candidate
    distance = lax.rem(place - source_place + size, size)
    forward, behind = device_at(place + 1), device_at(place - 1)
    barrier = pltpu.get_barrier_semaphore()
    for partner in (forward, behind):
        pl.semaphore_signal(barrier, inc=1, device_id={axis: partner}, device_id_type=MESH)
    pl.semaphore_wait(barrier, 2)
    piece = in_ref.shape[0] // (2 * chunks)

    def copy_of(way, chunk, ref):
        rows = pl.ds((way * chunks + chunk) * piece, piece)
        return pltpu.make_async_remote_copy(
            src_ref=ref.at[rows],
            dst_ref=out_ref.at[rows],
            send_sem=send_sem.at[way, chunk],
            recv_sem=recv_sem.at[way, chunk],
            device_id={axis: forward if way == 0 else behind},
            device_id_type=MESH,
        )

    @pl.when(distance == 0)
    def _():
        for chunk in range(chunks):
            for way in range(2):
                copy_of(way, chunk, in_ref).start()
        out_ref[...] = in_ref[...]
        for chunk in range(chunks):
            for way in range(2):
                copy_of(way, chunk, in_ref).wait_send()

    @pl.when(distance > 0)
    def _():
        for chunk in range(chunks):
            for way in range(2):
                hops = distance if way == 0 else size - distance
                copy_of(way, chunk, out_ref).wait_recv()

                @pl.when(hops < size - 1)
                def _():
                    copy_of(way, chunk, out_ref).start()

        for chunk in range(chunks):
            for way in range(2):
                hops = distance if way == 0 else size - distance

                @pl.when(hops < size - 1)
                def _():
                    copy_of(way, chunk, out_ref).wait_send()


def spread(block, axis, collective_id, chunks=8):
    size = lax.axis_size(axis)
    return pl.pallas_call(
        functools.partial(spread_kernel, axis, size, chunks),
        out_shape=jax.ShapeDtypeStruct(block.shape, block.dtype),
        in_specs=[pl.BlockSpec(memory_space=pltpu.VMEM)],
        out_specs=pl.BlockSpec(memory_space=pltpu.VMEM),
        scratch_shapes=[
            pltpu.SemaphoreType.DMA((2, chunks)),
            pltpu.SemaphoreType.DMA((2, chunks)),
        ],
        compiler_params=pltpu.CompilerParams(collective_id=collective_id, has_side_effects=True),
        name="spread",
    )(block)


def local(
    block_inputs,
    mixed_inputs,
    token_ids,
    target_ids,
    final_gain,
    out_weight,
    head_weight,
    out_master,
    out_first,
    out_second,
    head_master,
    head_first,
    head_second,
    embed_master,
    embed_first,
    embed_second,
):
    sections = lax.axis_size("section")
    replicas = lax.axis_size("dp")
    section = lax.axis_index("section")
    last = sections - 1
    batches, rows, width = mixed_inputs[0].shape
    tokens = batches * rows
    share = tokens // sections
    columns_own = width // replicas
    flat_mixed = mixed_inputs[0].reshape(tokens, width)
    all_mixed = lax.all_gather(flat_mixed, "dp", tiled=True)
    wide = block_inputs[0].reshape(tokens, width).astype(jnp.float32)
    slice_rows = head_weight.shape[0]
    vocabulary_start = section * slice_rows
    columns = vocabulary_start + lax.broadcasted_iota(jnp.int32, (1, slice_rows), 1)
    final = wide + times_transposed(flat_mixed, out_weight[0])
    final_inverse = lax.rsqrt(jnp.mean(final * final, axis=-1, keepdims=True) + norm_eps)
    own_hidden = (final * final_inverse * final_gain).astype(jnp.bfloat16)
    hidden = spread(own_hidden, "section", 0)
    logits = times_transposed(hidden, head_weight)
    local_top = jnp.max(logits, axis=1)
    local_weights = jnp.exp(logits - local_top[:, None])
    (stats,) = exchange(
        [jnp.stack([local_top, jnp.sum(local_weights, axis=1), final_inverse[:, 0]])],
        ["share"],
        "section",
        1,
    )
    row_top = jnp.max(stats[:, 0], axis=0)
    row_total = jnp.sum(stats[:, 1] * jnp.exp(stats[:, 0] - row_top), axis=0)
    predicted = local_weights * (jnp.exp(local_top - row_top) / row_total)[:, None]
    target_flat = target_ids.reshape(-1)
    logit_cotangent = jnp.where(target_flat[:, None] == columns, predicted - 1.0, predicted).astype(
        jnp.bfloat16
    )
    hidden_part = plain_times(logit_cotangent, head_weight).reshape(sections, share, width)
    (hidden_parts,) = exchange(
        [hidden_part], ["others"], "section", 2
    )
    hidden_cotangent = (
        lax.dynamic_index_in_dim(hidden_part, section, 0, False)
        + jnp.sum(hidden_parts, axis=0)
    )
    inverse = lax.dynamic_slice_in_dim(stats[last, 2], section * share, share)[:, None]
    unit = lax.dynamic_slice_in_dim(hidden, section * share, share).astype(jnp.float32) / final_gain
    scaled = hidden_cotangent * final_gain
    cotangent = (
        inverse * (scaled - unit * jnp.mean(scaled * unit, axis=-1, keepdims=True))
    ).astype(jnp.bfloat16)
    head_part = transposed_times(logit_cotangent, hidden)
    head_gradient = lax.psum_scatter(
        head_part, "dp", scatter_dimension=0, tiled=True
    )
    pieces = cotangent.reshape(share, replicas, columns_own).transpose(1, 0, 2)
    own_columns, all_tokens = exchange(
        [pieces, token_ids.reshape(1, tokens)], ["swap", "share"], "dp", 3
    )
    (all_columns,) = exchange([own_columns], ["share"], "section", 4)
    cotangent_columns = all_columns.transpose(1, 0, 2, 3).reshape(replicas * tokens, columns_own)
    marks = (all_tokens.reshape(-1, 1) == columns).astype(jnp.bfloat16)
    embed_columns = transposed_times(marks, cotangent_columns)
    (embed_parts,) = exchange(
        [embed_columns.reshape(replicas, slice_rows // replicas, columns_own)], ["swap"], "dp", 5
    )
    embed_gradient = (
        embed_parts.astype(jnp.float32).transpose(1, 0, 2).reshape(slice_rows // replicas, width)
    )
    out_gradient = transposed_times(cotangent_columns, all_mixed)
    out_out = adam_update(out_master, out_first, out_second, out_gradient.reshape(out_master.shape))
    head_out = adam_update(head_master, head_first, head_second, head_gradient)
    embed_out = adam_update(embed_master, embed_first, embed_second, embed_gradient)
    return out_out + head_out + embed_out


def solution(mesh):
    return jax.shard_map(
        local,
        mesh=mesh,
        in_specs=(
            P("section", None, "dp", None),
            P("section", None, "dp", None),
            P(None, "dp"),
            P(None, "dp"),
            P(),
            P("section", None, None),
            P("section", None),
            P("section", "dp", None),
            P("section", "dp", None),
            P("section", "dp", None),
            P(("section", "dp"), None),
            P(("section", "dp"), None),
            P(("section", "dp"), None),
            P(("section", "dp"), None),
            P(("section", "dp"), None),
            P(("section", "dp"), None),
        ),
        out_specs=(
            P("section", "dp", None),
            P("section", "dp", None),
            P("section", "dp", None),
            P(("section", "dp"), None),
            P(("section", "dp"), None),
            P(("section", "dp"), None),
            P(("section", "dp"), None),
            P(("section", "dp"), None),
            P(("section", "dp"), None),
        ),
        check_vma=False,
    )
```

time: 482 us -> 315 us (0.65)
  waiting for transfers between devices: 399 us -> 55.2 us
  Pallas kernels: 0 us -> 196 us
  blocking collectives: 15 us -> 0 us
  other arithmetic: 19 us -> 13.8 us
    reduce_scatter x3 -> x1, waiting for transfers between devices: 205 us -> 0.01 us  [local(): lax.psum_scatter(head_part, 'dp', scatter_dimension=0, tiled=True)]
    pallas_call x0 -> x6, Pallas kernels: none -> 196 us  [the longest x1 117 us: spread(): pl.pallas_call(functools.partial(spread_kernel, axis, size, chunks), out_...]
    psum x2 -> x0, waiting for transfers between devices: 119 us -> none  [the longest x1 64.4 us: local(): lax.psum(plain_times(logit_cotangent, head_weight), 'section')]
    ppermute x3 -> x0, waiting for transfers between devices: 74.7 us -> none  [from_behind(): return lax.ppermute(block, axis, route)]
    all_gather x0 -> x1, waiting for transfers between devices: none -> 54.5 us  [local(): all_mixed = lax.all_gather(flat_mixed, 'dp', tiled=True)]
    all_gather x2 -> x0, blocking collectives: 15 us -> none  [combined_all(): gathered = jax.tree.map(lambda a: lax.all_gather(a, axis), part)]
    sub x3 -> x2, other arithmetic: 12.3 us -> 5.59 us  [adam_update(): master - learning_rate * (first_next / (jnp.sqrt(second_next) + adam_eps)...]
  transfers between devices with their start and end apart: 8 -> 2, of which waited for: 7 -> 1; matrix products, arithmetic and copies ran while one was open for 5% -> 6% of each run, Pallas kernels for 0% -> 23%
where the time goes in v1:
time: 315 us; the launch traced here: 314 us
  Pallas kernels  196 us (62%)
  waiting for transfers between devices  55.2 us (18%)
  matrix products  28.8 us (9%)
  between operations  14.2 us (5%)
  other arithmetic  13.8 us (4%)
  local copies, waits for them, and re-layouts  5.49 us (2%)
    pallas_call x1, Pallas kernels, spread(): pl.pallas_call(functools.partial(spread_kernel, axis, size, chunks), out_...  117 us
    pallas_call x5, Pallas kernels, exchange(): pl.pallas_call(functools.partial(exchange_kernel, axis, size, tuple(modes...  79.8 us
    all_gather x1, waiting for transfers between devices, local(): all_mixed = lax.all_gather(flat_mixed, 'dp', tiled=True)  54.5 us
    dot_general x3, matrix products, transposed_times(): lax.dot_general(former, latter, (((0,), (0,)), ((), ())), preferred_eleme...  17 us
    dot_general x2, matrix products, times_transposed(): lax.dot_general(former, latter, (((1,), (1,)), ((), ())), preferred_eleme...  8.68 us
  transfers between devices with their start and end apart: 2, of which 1 were waited for; matrix products, arithmetic and copies ran while one was open for 6% of the time, Pallas kernels for 23%

profile of v1, /device:TPU:0, one launch (start us, length us, event | category | flops | bytes accessed | tf_op | source)
XLA Modules:
  0.0 314.1 jit_solution(9703628783470577024)
XLA Ops:
  7.3 6.5 %multiply_reduce_fusion = (f32[256]{0:T(256)S(1)}, f32[256,2048]{1,0:T(8,128)S(1)}) fusion(bf16[256,2048]{1,0:T(8,128)(2,1)} %bitcast.75, bf16[1,2048,2048]{2,1,0:T(8,128)(2,1)} %param.21, bf16[256,2048]{1,0:T(8,128)(2,1)} %bitcast.82), kind=kOutput, calls=%fused_computation.13 | convolution fusion | flops 2149580544 | bytes 12583936 | tf_op jit(solution)/shard_map/dot_general | solution.py:20
  13.8 1.2 multiply_convert_fusion.in_ref
  15.0 116.7 %spread.1 = bf16[256,2048]{1,0:T(8,128)(2,1)} custom-call(bf16[256,2048]{1,0:T(8,128)(2,1)} %multiply_convert_fusion.in_ref), custom_call_target="tpu_custom_call" | custom-call | tf_op jit(solution)/shard_map/spread/pallas_call | solution.py:168
  131.7 2.1 fusion.28
  133.9 0.8 copy-done.2
  135.5 6.9 %shard_map.223 = f32[4,3,256]{2,1,0:T(4,128)} custom-call(f32[3,256]{1,0:T(4,128)} %pad_maximum_fusion.refs_0_), custom_call_target="tpu_custom_call" | custom-call | tf_op jit(solution)/shard_map/pallas_call | solution.py:86
  142.4 0.8 slice_reduce_fusion
  143.4 3.9 %fusion.21 = f32[512,2048]{1,0:T(8,128)} fusion(bf16[256,2048]{1,0:T(8,128)(2,1)S(1)} %copy-done.1, f32[256,512]{1,0:T(8,128)} %copy-done.2, f32[256]{0:T(256)S(1)} %exponential_divide_fusion, s32[512]{0:T(512)S(1)} %iota_add_fusion, f32[256]{0:T(256)S(1)} %get-tuple-element.27, s32[256]{0:T(256)S(1)} %eq.36), kind=kOutput, calls=%fused_computation.46 | convolution fusion | flops 537657344 | bytes 5772288 | tf_op jit(solution)/shard_map/dot_general | solution.py:26
  148.8 3.2 %fusion.23 = f32[256,2048]{1,0:T(8,128)} fusion(bf16[512,2048]{1,0:T(8,128)(2,1)S(1)} %copy-done, f32[256,512]{1,0:T(8,128)} %copy-done.2, f32[256]{0:T(256)S(1)} %exponential_divide_fusion, s32[512]{0:T(512)S(1)} %iota_add_fusion, f32[256]{0:T(256)S(1)} %get-tuple-element.27, s32[256]{0:T(256)S(1)} %eq.36), kind=kOutput, calls=%fused_computation.47 | convolution fusion | flops 537657344 | bytes 4723712 | tf_op jit(solution)/shard_map/dot_general | solution.py:32
  152.0 18.5 %shard_map.224 = f32[3,64,2048]{2,1,0:T(8,128)} custom-call(f32[4,64,2048]{2,1,0:T(8,128)} %bitcast.67), custom_call_target="tpu_custom_call" | custom-call | tf_op jit(solution)/shard_map/pallas_call | solution.py:86
  170.5 2.4 reduce_sum.48
  173.0 1.4 multiply_reduce_fusion.1
  174.4 1.4 multiply_convert_fusion.1
  175.9 0.7 copy.46
  177.2 15.1 %shard_map.225 = (bf16[8,64,256]{2,1,0:T(8,128)(2,1)}, s32[8,1,256]{2,1,0:T(1,128)}) custom-call(bf16[8,64,256]{2,1,0:T(8,128)(2,1)} %bitcast.77, s32[1,256]{1,0:T(1,128)} %reshape.109.refs_1_), custom_call_target="tpu_custom_call" | custom-call | tf_op jit(solution)/shard_map/pallas_call | solution.py:86
  192.4 15.7 %shard_map.226 = bf16[4,8,64,256]{3,2,1,0:T(8,128)(2,1)} custom-call(bf16[8,64,256]{2,1,0:T(8,128)(2,1)} %get-tuple-element.11.refs_0_), custom_call_target="tpu_custom_call" | custom-call | tf_op jit(solution)/shard_map/pallas_call | solution.py:86
  208.1 1.4 copy.28
  209.5 1.6 fusion.2.refs_0_
  211.0 23.5 %shard_map.227 = f32[8,64,256]{2,1,0:T(8,128)} custom-call(f32[8,64,256]{2,1,0:T(8,128)} %fusion.2.refs_0_), custom_call_target="tpu_custom_call" | custom-call | tf_op jit(solution)/shard_map/pallas_call | solution.py:86
  234.6 1.1 copy.34
  235.7 2.7 multiply_subtract_fusion.1
  238.4 2.9 multiply_subtract_fusion.2
  241.3 54.5 %all-gather.2.cloned.1.call-done = bf16[2048,2048]{1,0:T(8,128)(2,1)} async-done(((bf16[256,2048]{1,0:T(8,128)(2,1)}), bf16[2048,2048]{1,0:T(8,128)(2,1)}) %all-gather.2.cloned.1.call-update) | async-done | bytes 8388624 | tf_op jit(solution)/shard_map/all_gather | solution.py:209
  295.8 11.5 %multiply_subtract_fusion = (f32[1,256,2048]{2,1,0:T(8,128)}, f32[1,256,2048]{2,1,0:T(8,128)}, f32[1,256,2048]{2,1,0:T(8,128)}) fusion(f32[1,256,2048]{2,1,0:T(8,128)} %param.23, f32[1,256,2048]{2,1,0:T(8,128)} %param.25, f32[1,256,2048]{2,1,0:T(8,128)} %param.24, bf16[2048,256]{1,0:T(8,128)(2,1)S(1)} %bitcast.71, ...), kind=kOutput, calls=%fused_computation.11 | convolution fusion | flops 2154299392 | bytes 22020096 | tf_op jit(solution)/shard_map/dot_general | solution.py:26
  (30 shorter events, 3.2 us)
Async XLA Ops:
  7.2 124.5 %copy-start = (bf16[512,2048]{1,0:T(8,128)(2,1)S(1)}, bf16[512,2048]{1,0:T(8,128)(2,1)}, u32[]{:S(2)}) copy-start(bf16[512,2048]{1,0:T(8,128)(2,1)} %param.22) | copy-start | bytes 6291460
  7.2 231.2 %reduce-scatter.2.cloned.1.call-start = ((), (), s32[]{:S(2)}) async-start(), calls=%async_computation.2 | async-start | bytes 4718592 | tf_op jit(solution)/shard_map/reduce_scatter | solution.py:249
  7.2 6.6 %copy-start.3 = (f32[2048]{0:T(1024)S(1)}, f32[2048]{0:T(1024)}, u32[]{:S(2)}) copy-start(f32[2048]{0:T(1024)} %param.20) | copy-start | bytes 24580
  131.7 11.6 %copy-start.4 = (s32[4,64]{1,0:T(4,128)S(1)}, s32[4,64]{1,0:T(4,128)}, u32[]{:S(2)}) copy-start(s32[4,64]{1,0:T(4,128)} %param.19) | copy-start | bytes 3076
  131.7 11.7 %copy-start.1 = (bf16[256,2048]{1,0:T(8,128)(2,1)S(1)}, bf16[256,2048]{1,0:T(8,128)(2,1)}, u32[]{:S(2)}) copy-start(bf16[256,2048]{1,0:T(8,128)(2,1)} %spread.1) | copy-start | bytes 3145732
  133.9 0.8 copy-start.2
  147.4 148.4 %all-gather.2.cloned.1.call-start = ((), (), s32[]{:S(2)}) async-start(), calls=%async_computation.1 | async-start | bytes 9437184 | tf_op jit(solution)/shard_map/all_gather | solution.py:209
  172.9 3.7 %copy-start.5 = (s32[4,64]{1,0:T(4,128)S(1)}, s32[4,64]{1,0:T(4,128)}, u32[]{:S(2)}) copy-start(s32[4,64]{1,0:T(4,128)} %param.18) | copy-start | bytes 3076
  192.3 17.1 %copy-start.6 = (s32[8,1,256]{2,1,0:T(1,128)S(1)}, s32[8,1,256]{2,1,0:T(1,128)}, u32[]{:S(2)}) copy-start(s32[8,1,256]{2,1,0:T(1,128)} %get-tuple-element.12) | copy-start | bytes 24580
Sparse Core Ops, SparseCore 0:
  147.5 54.5 reduce-scatter.1
  203.7 92.0 all-gather.1

commit v2 on v1

--- a/solution.py
+++ b/solution.py
@@ -96,83 +96,64 @@
     )(*arrays)
 
 
-def spread_kernel(axis, size, chunks, in_ref, out_ref, send_sem, recv_sem):
+def spread_kernel(axis, size, in_ref, out_ref, send_sem, recv_sem):
     me = lax.axis_index(axis)
-    place = me
-    shift = me // 2
-    while_size = size
-    while while_size > 2:
-        place = place ^ shift
-        shift = shift // 2
-        while_size //= 2
-
-    def device_at(position):
-        position = lax.rem(position + size, size)
-        return position ^ (position // 2)
-
-    source_place = 0
-    for candidate in range(size):
-        if candidate ^ (candidate // 2) == size - 1:
-            source_place = candidate
-    distance = lax.rem(place - source_place + size, size)
-    forward, behind = device_at(place + 1), device_at(place - 1)
-    barrier = pltpu.get_barrier_semaphore()
-    for partner in (forward, behind):
-        pl.semaphore_signal(barrier, inc=1, device_id={axis: partner}, device_id_type=MESH)
-    pl.semaphore_wait(barrier, 2)
-    piece = in_ref.shape[0] // (2 * chunks)
-
-    def copy_of(way, chunk, ref):
-        rows = pl.ds((way * chunks + chunk) * piece, piece)
+    last = size - 1
+    second = last // 2
+    piece = in_ref.shape[0] // size
+    greet(axis, size, me)
+
+    def copy_of(part, target, ref):
+        rows = pl.ds(part * piece, piece)
         return pltpu.make_async_remote_copy(
             src_ref=ref.at[rows],
             dst_ref=out_ref.at[rows],
-            send_sem=send_sem.at[way, chunk],
-            recv_sem=recv_sem.at[way, chunk],
-            device_id={axis: forward if way == 0 else behind},
+            send_sem=send_sem.at[part, target],
+            recv_sem=recv_sem.at[part],
+            device_id={axis: target},
             device_id_type=MESH,
         )
 
-    @pl.when(distance == 0)
+    def relayed(device):
+        return [device, last] if device == second else [device]
+
+    @pl.when(me == last)
     def _():
-        for chunk in range(chunks):
-            for way in range(2):
-                copy_of(way, chunk, in_ref).start()
+        copies = [copy_of(part, k, in_ref) for k in range(last) for part in relayed(k)]
+        for copy in copies:
+            copy.start()
         out_ref[...] = in_ref[...]
-        for chunk in range(chunks):
-            for way in range(2):
-                copy_of(way, chunk, in_ref).wait_send()
-
-    @pl.when(distance > 0)
-    def _():
-        for chunk in range(chunks):
-            for way in range(2):
-                hops = distance if way == 0 else size - distance
-                copy_of(way, chunk, out_ref).wait_recv()
-
-                @pl.when(hops < size - 1)
-                def _():
-                    copy_of(way, chunk, out_ref).start()
-
-        for chunk in range(chunks):
-            for way in range(2):
-                hops = distance if way == 0 else size - distance
-
-                @pl.when(hops < size - 1)
-                def _():
-                    copy_of(way, chunk, out_ref).wait_send()
-
-
-def spread(block, axis, collective_id, chunks=8):
+        for copy in copies:
+            copy.wait_send()
+
+    for device in range(last):
+
+        @pl.when(me == device)
+        def _():
+            others = [k for k in range(last) if k != device]
+            copies = []
+            for part in relayed(device):
+                copy_of(part, others[0], out_ref).wait_recv()
+                for k in others:
+                    copies.append(copy_of(part, k, out_ref))
+                    copies[-1].start()
+            for part in range(size):
+                if part not in relayed(device):
+                    copy_of(part, others[0], out_ref).wait_recv()
+            for copy in copies:
+                copy.wait_send()
+
+
+def spread(block, axis, collective_id):
     size = lax.axis_size(axis)
     return pl.pallas_call(
-        functools.partial(spread_kernel, axis, size, chunks),
+        functools.partial(spread_kernel, axis, size),
         out_shape=jax.ShapeDtypeStruct(block.shape, block.dtype),
         in_specs=[pl.BlockSpec(memory_space=pltpu.VMEM)],
         out_specs=pl.BlockSpec(memory_space=pltpu.VMEM),
         scratch_shapes=[
-            pltpu.SemaphoreType.DMA((2, chunks)),
-            pltpu.SemaphoreType.DMA((2, chunks)),
+            pltpu.SemaphoreType.DMA((size, size)),
+            pltpu.SemaphoreType.DMA((size,)),
         ],
         compiler_params=pltpu.CompilerParams(collective_id=collective_id, has_side_effects=True),
         name="spread",

time: 315 us -> 233 us (0.74)
  Pallas kernels: 196 us -> 121 us
  waiting for transfers between devices: 55.2 us -> 48.9 us
    pallas_call x1, Pallas kernels: 117 us -> 32.9 us  [spread(): pl.pallas_call(functools.partial(spread_kernel, axis, size), out_shape=ja...]
    pallas_call x5, Pallas kernels: 79.8 us -> 88 us  [exchange(): pl.pallas_call(functools.partial(exchange_kernel, axis, size, tuple(modes...]
    all_gather x1, waiting for transfers between devices: 54.5 us -> 48.2 us  [local(): all_mixed = lax.all_gather(flat_mixed, 'dp', tiled=True)]
  transfers between devices with their start and end apart: 2 -> 2, of which waited for: 1 -> 1; matrix products, arithmetic and copies ran while one was open for 6% -> 9% of each run, Pallas kernels for 23% -> 34%
where the time goes in v2:
time: 233 us; the launch traced here: 232 us
  Pallas kernels  121 us (52%)
  waiting for transfers between devices  48.9 us (21%)
  matrix products  28.8 us (12%)
  between operations  14.2 us (6%)
  other arithmetic  13.7 us (6%)
  local copies, waits for them, and re-layouts  5.4 us (2%)
    pallas_call x5, Pallas kernels, exchange(): pl.pallas_call(functools.partial(exchange_kernel, axis, size, tuple(modes...  88 us
    all_gather x1, waiting for transfers between devices, local(): all_mixed = lax.all_gather(flat_mixed, 'dp', tiled=True)  48.2 us
    pallas_call x1, Pallas kernels, spread(): pl.pallas_call(functools.partial(spread_kernel, axis, size), out_shape=ja...  32.9 us
    dot_general x3, matrix products, transposed_times(): lax.dot_general(former, latter, (((0,), (0,)), ((), ())), preferred_eleme...  17 us
    dot_general x2, matrix products, times_transposed(): lax.dot_general(former, latter, (((1,), (1,)), ((), ())), preferred_eleme...  8.69 us
    sub x2, other arithmetic, adam_update(): master - learning_rate * (first_next / (jnp.sqrt(second_next) + adam_eps)...  5.59 us
  transfers between devices with their start and end apart: 2, of which 1 were waited for; matrix products, arithmetic and copies ran while one was open for 9% of the time, Pallas kernels for 34%

profile of v2, /device:TPU:0, one launch (start us, length us, event | category | flops | bytes accessed | tf_op | source)
XLA Modules:
  0.0 232.2 jit_solution(13884107521848995771)
XLA Ops:
  7.3 6.5 %multiply_reduce_fusion = (f32[256]{0:T(256)S(1)}, f32[256,2048]{1,0:T(8,128)S(1)}) fusion(bf16[256,2048]{1,0:T(8,128)(2,1)} %bitcast.75, bf16[1,2048,2048]{2,1,0:T(8,128)(2,1)} %param.21, bf16[256,2048]{1,0:T(8,128)(2,1)} %bitcast.82), kind=kOutput, calls=%fused_computation.13 | convolution fusion | flops 2149580544 | bytes 12583936 | tf_op jit(solution)/shard_map/dot_general | solution.py:20
  13.8 1.2 multiply_convert_fusion.in_ref
  15.0 32.9 %spread.1 = bf16[256,2048]{1,0:T(8,128)(2,1)} custom-call(bf16[256,2048]{1,0:T(8,128)(2,1)} %multiply_convert_fusion.in_ref), custom_call_target="tpu_custom_call" | custom-call | tf_op jit(solution)/shard_map/spread/pallas_call | solution.py:149
  48.0 2.1 fusion.28
  50.2 0.8 copy-done.2
  51.8 8.7 %shard_map.223 = f32[4,3,256]{2,1,0:T(4,128)} custom-call(f32[3,256]{1,0:T(4,128)} %pad_maximum_fusion.refs_0_), custom_call_target="tpu_custom_call" | custom-call | tf_op jit(solution)/shard_map/pallas_call | solution.py:86
  60.5 0.8 slice_reduce_fusion
  61.4 3.9 %fusion.21 = f32[512,2048]{1,0:T(8,128)} fusion(bf16[256,2048]{1,0:T(8,128)(2,1)S(1)} %copy-done.1, f32[256,512]{1,0:T(8,128)} %copy-done.2, f32[256]{0:T(256)S(1)} %exponential_divide_fusion, s32[512]{0:T(512)S(1)} %iota_add_fusion, f32[256]{0:T(256)S(1)} %get-tuple-element.27, s32[256]{0:T(256)S(1)} %eq.36), kind=kOutput, calls=%fused_computation.46 | convolution fusion | flops 537657344 | bytes 5772288 | tf_op jit(solution)/shard_map/dot_general | solution.py:26
  66.9 3.2 %fusion.23 = f32[256,2048]{1,0:T(8,128)} fusion(bf16[512,2048]{1,0:T(8,128)(2,1)S(1)} %copy-done, f32[256,512]{1,0:T(8,128)} %copy-done.2, f32[256]{0:T(256)S(1)} %exponential_divide_fusion, s32[512]{0:T(512)S(1)} %iota_add_fusion, f32[256]{0:T(256)S(1)} %get-tuple-element.27, s32[256]{0:T(256)S(1)} %eq.36), kind=kOutput, calls=%fused_computation.47 | convolution fusion | flops 537657344 | bytes 4723712 | tf_op jit(solution)/shard_map/dot_general | solution.py:32
  70.0 24.6 %shard_map.224 = f32[3,64,2048]{2,1,0:T(8,128)} custom-call(f32[4,64,2048]{2,1,0:T(8,128)} %bitcast.67), custom_call_target="tpu_custom_call" | custom-call | tf_op jit(solution)/shard_map/pallas_call | solution.py:86
  94.7 2.4 %reduce_sum.48 = f32[64,2048]{1,0:T(8,128)} reduce(f32[3,64,2048]{2,1,0:T(8,128)} %shard_map.224, f32[]{:T(128)} %constant.17.clone.1), dimensions={0}, to_apply=%region_5.6 | reduce | flops 262144 | bytes 2097156 | tf_op jit(solution)/shard_map/reduce_sum | solution.py:221
  97.1 1.4 multiply_reduce_fusion.1
  98.5 1.4 multiply_convert_fusion.1
  100.0 0.7 copy.46
  101.4 14.6 %shard_map.225 = (bf16[8,64,256]{2,1,0:T(8,128)(2,1)}, s32[8,1,256]{2,1,0:T(1,128)}) custom-call(bf16[8,64,256]{2,1,0:T(8,128)(2,1)} %bitcast.77, s32[1,256]{1,0:T(1,128)} %reshape.109.refs_1_), custom_call_target="tpu_custom_call" | custom-call | tf_op jit(solution)/shard_map/pallas_call | solution.py:86
  116.0 16.2 %shard_map.226 = bf16[4,8,64,256]{3,2,1,0:T(8,128)(2,1)} custom-call(bf16[8,64,256]{2,1,0:T(8,128)(2,1)} %get-tuple-element.11.refs_0_), custom_call_target="tpu_custom_call" | custom-call | tf_op jit(solution)/shard_map/pallas_call | solution.py:86
  132.2 1.3 copy.28
  133.5 1.6 fusion.2.refs_0_
  135.1 23.9 %shard_map.227 = f32[8,64,256]{2,1,0:T(8,128)} custom-call(f32[8,64,256]{2,1,0:T(8,128)} %fusion.2.refs_0_), custom_call_target="tpu_custom_call" | custom-call | tf_op jit(solution)/shard_map/pallas_call | solution.py:86
  158.9 1.1 copy.34
  160.0 2.7 %multiply_subtract_fusion.1 = (f32[64,2048]{1,0:T(8,128)}, f32[64,2048]{1,0:T(8,128)}, f32[64,2048]{1,0:T(8,128)}) fusion(f32[64,2048]{1,0:T(8,128)} %param.29, f32[64,2048]{1,0:T(8,128)S(1)} %bitcast.73, f32[64,2048]{1,0:T(8,128)} %param.31, f32[64,2048]{1,0:T(8,128)} %param.30), kind=kLoop, calls=%fused_computation.22 | loop fusion | flops 1703936 | bytes 3670016 | tf_op jit(solution)/shard_map/sub | solution.py:38
  162.8 2.9 %multiply_subtract_fusion.2 = (f32[64,2048]{1,0:T(8,128)}, f32[64,2048]{1,0:T(8,128)}, f32[64,2048]{1,0:T(8,128)}) fusion(f32[64,2048]{1,0:T(8,128)} %param.26, f32[64,2048]{1,0:T(8,128)} %reduce-scatter.2.cloned.1.call-done, f32[64,2048]{1,0:T(8,128)} %param.28, f32[64,2048]{1,0:T(8,128)} %param.27), kind=kLoop, calls=%fused_computation.24 | loop fusion | flops 1703936 | bytes 3670016 | tf_op jit(solution)/shard_map/sub | solution.py:38
  165.6 48.2 %all-gather.2.cloned.1.call-done = bf16[2048,2048]{1,0:T(8,128)(2,1)} async-done(((bf16[256,2048]{1,0:T(8,128)(2,1)}), bf16[2048,2048]{1,0:T(8,128)(2,1)}) %all-gather.2.cloned.1.call-update) | async-done | bytes 8388624 | tf_op jit(solution)/shard_map/all_gather | solution.py:190
  213.9 11.5 %multiply_subtract_fusion = (f32[1,256,2048]{2,1,0:T(8,128)}, f32[1,256,2048]{2,1,0:T(8,128)}, f32[1,256,2048]{2,1,0:T(8,128)}) fusion(f32[1,256,2048]{2,1,0:T(8,128)} %param.23, f32[1,256,2048]{2,1,0:T(8,128)} %param.25, f32[1,256,2048]{2,1,0:T(8,128)} %param.24, bf16[2048,256]{1,0:T(8,128)(2,1)S(1)} %bitcast.71, ...), kind=kOutput, calls=%fused_computation.11 | convolution fusion | flops 2154299392 | bytes 22020096 | tf_op jit(solution)/shard_map/dot_general | solution.py:26
  (30 shorter events, 3.2 us)
Async XLA Ops:
  7.2 40.8 %copy-start = (bf16[512,2048]{1,0:T(8,128)(2,1)S(1)}, bf16[512,2048]{1,0:T(8,128)(2,1)}, u32[]{:S(2)}) copy-start(bf16[512,2048]{1,0:T(8,128)(2,1)} %param.22) | copy-start | bytes 6291460
  7.2 155.6 %reduce-scatter.2.cloned.1.call-start = ((), (), s32[]{:S(2)}) async-start(), calls=%async_computation.2 | async-start | bytes 4718592 | tf_op jit(solution)/shard_map/reduce_scatter | solution.py:230
  7.2 6.6 %copy-start.3 = (f32[2048]{0:T(1024)S(1)}, f32[2048]{0:T(1024)}, u32[]{:S(2)}) copy-start(f32[2048]{0:T(1024)} %param.20) | copy-start | bytes 24580
  48.0 13.4 %copy-start.4 = (s32[4,64]{1,0:T(4,128)S(1)}, s32[4,64]{1,0:T(4,128)}, u32[]{:S(2)}) copy-start(s32[4,64]{1,0:T(4,128)} %param.19) | copy-start | bytes 3076
  48.0 13.5 %copy-start.1 = (bf16[256,2048]{1,0:T(8,128)(2,1)S(1)}, bf16[256,2048]{1,0:T(8,128)(2,1)}, u32[]{:S(2)}) copy-start(bf16[256,2048]{1,0:T(8,128)(2,1)} %spread.1) | copy-start | bytes 3145732
  50.1 0.8 copy-start.2
  65.4 148.4 %all-gather.2.cloned.1.call-start = ((), (), s32[]{:S(2)}) async-start(), calls=%async_computation.1 | async-start | bytes 9437184 | tf_op jit(solution)/shard_map/all_gather | solution.py:190
  97.0 3.7 %copy-start.5 = (s32[4,64]{1,0:T(4,128)S(1)}, s32[4,64]{1,0:T(4,128)}, u32[]{:S(2)}) copy-start(s32[4,64]{1,0:T(4,128)} %param.18) | copy-start | bytes 3076
  116.0 17.5 %copy-start.6 = (s32[8,1,256]{2,1,0:T(1,128)S(1)}, s32[8,1,256]{2,1,0:T(1,128)}, u32[]{:S(2)}) copy-start(s32[8,1,256]{2,1,0:T(1,128)} %get-tuple-element.12) | copy-start | bytes 24580
Sparse Core Ops, SparseCore 0:
  65.5 54.5 reduce-scatter.1
  121.7 92.1 all-gather.1

commit v3 on v2

--- a/solution.py
+++ b/solution.py
@@ -238,9 +238,14 @@
     cotangent_columns = all_columns.transpose(1, 0, 2, 3).reshape(replicas * tokens, columns_own)
     marks = (all_tokens.reshape(-1, 1) == columns).astype(jnp.bfloat16)
     embed_columns = transposed_times(marks, cotangent_columns)
-    (embed_parts,) = exchange(
-        [embed_columns.reshape(replicas, slice_rows // replicas, columns_own)], ["swap"], "dp", 5
-    )
+    embed_blocks = embed_columns.reshape(replicas, slice_rows // replicas, columns_own)
+    replica = lax.axis_index("dp")
+    embed_steps = []
+    for step in range(replicas):
+        block = lax.dynamic_index_in_dim(embed_blocks, (replica + step) % replicas, 0, False)
+        route = [(i, (i + step) % replicas) for i in range(replicas)]
+        embed_steps.append(lax.ppermute(block, "dp", route) if step else block)
+    embed_parts = jnp.roll(jnp.stack(embed_steps[::-1]), replica + 1, axis=0)
     embed_gradient = (
         embed_parts.astype(jnp.float32).transpose(1, 0, 2).reshape(slice_rows // replicas, width)
     )

time: 233 us -> 233 us (level)
  Pallas kernels: 121 us -> 97 us
  waiting for transfers between devices: 48.9 us -> 65.2 us
  starting transfers between devices: 0.08 us -> 7.33 us
  local copies, waits for them, and re-layouts: 5.4 us -> 7.76 us
    ppermute x0 -> x7, waiting for transfers between devices: none -> 24.8 us  [local(): embed_steps.append(lax.ppermute(block, 'dp', route) if step else block)]
    pallas_call x5 -> x4, Pallas kernels: 88 us -> 64.1 us  [exchange(): pl.pallas_call(functools.partial(exchange_kernel, axis, size, tuple(modes...]
    all_gather x1, waiting for transfers between devices: 48.2 us -> 39.7 us  [local(): all_mixed = lax.all_gather(flat_mixed, 'dp', tiled=True)]
    ppermute x0 -> x7, starting transfers between devices: none -> 7.25 us  [local(): embed_steps.append(lax.ppermute(block, 'dp', route) if step else block)]
  transfers between devices with their start and end apart: 2 -> 9, of which waited for: 1 -> 5; matrix products, arithmetic and copies ran while one was open for 9% -> 8% of each run, Pallas kernels for 34% -> 24%
where the time goes in v3:
time: 233 us; the launch traced here: 232 us
  Pallas kernels  97 us (42%)
  waiting for transfers between devices  65.2 us (28%)
  matrix products  28 us (12%)
  between operations  14.4 us (6%)
  other arithmetic  12.4 us (5%)
  local copies, waits for them, and re-layouts  7.76 us (3%)
  starting transfers between devices  7.33 us (3%)
    pallas_call x4, Pallas kernels, exchange(): pl.pallas_call(functools.partial(exchange_kernel, axis, size, tuple(modes...  64.1 us
    all_gather x1, waiting for transfers between devices, local(): all_mixed = lax.all_gather(flat_mixed, 'dp', tiled=True)  39.7 us
    pallas_call x1, Pallas kernels, spread(): pl.pallas_call(functools.partial(spread_kernel, axis, size), out_shape=ja...  32.9 us
    ppermute x7, waiting for transfers between devices, local(): embed_steps.append(lax.ppermute(block, 'dp', route) if step else block)  24.8 us
    dot_general x3, matrix products, transposed_times(): lax.dot_general(former, latter, (((0,), (0,)), ((), ())), preferred_eleme...  16.2 us
    dot_general x2, matrix products, times_transposed(): lax.dot_general(former, latter, (((1,), (1,)), ((), ())), preferred_eleme...  8.68 us
    ppermute x7, starting transfers between devices, local(): embed_steps.append(lax.ppermute(block, 'dp', route) if step else block)  7.25 us
  transfers between devices with their start and end apart: 9, of which 5 were waited for; matrix products, arithmetic and copies ran while one was open for 8% of the time, Pallas kernels for 24%

profile of v3, /device:TPU:0, one launch (start us, length us, event | category | flops | bytes accessed | tf_op | source)
XLA Modules:
  0.0 232.1 jit_solution(11593341062209095152)
XLA Ops:
  7.3 6.5 %multiply_reduce_fusion = (f32[256]{0:T(256)S(1)}, f32[256,2048]{1,0:T(8,128)S(1)}) fusion(bf16[256,2048]{1,0:T(8,128)(2,1)} %bitcast.110, bf16[1,2048,2048]{2,1,0:T(8,128)(2,1)} %param.21, bf16[256,2048]{1,0:T(8,128)(2,1)} %bitcast.117), kind=kOutput, calls=%fused_computation.13 | convolution fusion | flops 2149580544 | bytes 12583936 | tf_op jit(solution)/shard_map/dot_general | solution.py:20
  13.8 1.2 multiply_convert_fusion.in_ref
  15.0 32.9 %spread.1 = bf16[256,2048]{1,0:T(8,128)(2,1)} custom-call(bf16[256,2048]{1,0:T(8,128)(2,1)} %multiply_convert_fusion.in_ref), custom_call_target="tpu_custom_call" | custom-call | tf_op jit(solution)/shard_map/spread/pallas_call | solution.py:149
  48.0 2.1 fusion.28
  51.7 8.7 %shard_map.223 = f32[4,3,256]{2,1,0:T(4,128)} custom-call(f32[3,256]{1,0:T(4,128)} %pad_maximum_fusion.refs_0_), custom_call_target="tpu_custom_call" | custom-call | tf_op jit(solution)/shard_map/pallas_call | solution.py:86
  61.4 3.9 %fusion.21 = f32[512,2048]{1,0:T(8,128)} fusion(bf16[256,2048]{1,0:T(8,128)(2,1)S(1)} %copy-done.1, f32[256,512]{1,0:T(8,128)} %copy-done.2, f32[256]{0:T(256)S(1)} %exponential_divide_fusion, s32[512]{0:T(512)S(1)} %iota_add_fusion, f32[256]{0:T(256)S(1)} %get-tuple-element.34, s32[256]{0:T(256)S(1)} %eq.48), kind=kOutput, calls=%fused_computation.70 | convolution fusion | flops 537657344 | bytes 5772288 | tf_op jit(solution)/shard_map/dot_general | solution.py:26
  66.8 3.2 %fusion.23 = f32[256,2048]{1,0:T(8,128)} fusion(bf16[512,2048]{1,0:T(8,128)(2,1)S(1)} %copy-done, f32[256,512]{1,0:T(8,128)} %copy-done.2, f32[256]{0:T(256)S(1)} %exponential_divide_fusion, s32[512]{0:T(512)S(1)} %iota_add_fusion, f32[256]{0:T(256)S(1)} %get-tuple-element.34, s32[256]{0:T(256)S(1)} %eq.48), kind=kOutput, calls=%fused_computation.71 | convolution fusion | flops 537657344 | bytes 4723712 | tf_op jit(solution)/shard_map/dot_general | solution.py:32
  70.0 24.6 %shard_map.224 = f32[3,64,2048]{2,1,0:T(8,128)} custom-call(f32[4,64,2048]{2,1,0:T(8,128)} %bitcast.103), custom_call_target="tpu_custom_call" | custom-call | tf_op jit(solution)/shard_map/pallas_call | solution.py:86
  94.6 2.4 %reduce_sum.48 = f32[64,2048]{1,0:T(8,128)} reduce(f32[3,64,2048]{2,1,0:T(8,128)} %shard_map.224, f32[]{:T(128)} %constant.114.clone.1), dimensions={0}, to_apply=%region_5.6 | reduce | flops 262144 | bytes 2097156 | tf_op jit(solution)/shard_map/reduce_sum | solution.py:221
  97.0 1.4 multiply_reduce_fusion.1
  98.5 1.4 multiply_convert_fusion.1
  101.3 14.6 %shard_map.225 = (bf16[8,64,256]{2,1,0:T(8,128)(2,1)}, s32[8,1,256]{2,1,0:T(1,128)}) custom-call(bf16[8,64,256]{2,1,0:T(8,128)(2,1)} %bitcast.112, s32[1,256]{1,0:T(1,128)} %reshape.109.refs_1_), custom_call_target="tpu_custom_call" | custom-call | tf_op jit(solution)/shard_map/pallas_call | solution.py:86
  115.9 16.2 %shard_map.226 = bf16[4,8,64,256]{3,2,1,0:T(8,128)(2,1)} custom-call(bf16[8,64,256]{2,1,0:T(8,128)(2,1)} %get-tuple-element.11.refs_0_), custom_call_target="tpu_custom_call" | custom-call | tf_op jit(solution)/shard_map/pallas_call | solution.py:86
  132.1 1.3 copy.29
  135.8 4.1 %collective-permute-start = (f32[64,256]{1,0:T(8,128)}, f32[64,256]{1,0:T(8,128)S(1)}, u32[]{:S(2)}, u32[]{:S(2)}) collective-permute-start(f32[64,256]{1,0:T(8,128)} %get-tuple-element.28), channel_id=1, source_target_pairs={{0,7},{1,0},{2,1},{3,2},{4,3},{5,4},{6,5},{7,6},{8,15},{9,8},{10,9... | collective-permute-start | bytes 196616 | tf_op jit(solution)/shard_map/ppermute | solution.py:247
  140.3 2.2 collective-permute-start.3
  142.5 1.5 collective-permute-done
  144.6 4.7 %collective-permute-done.1 = f32[64,256]{1,0:T(8,128)S(1)} collective-permute-done((f32[64,256]{1,0:T(8,128)}, f32[64,256]{1,0:T(8,128)S(1)}, u32[]{:S(2)}, u32[]{:S(2)}) %collective-permute-start.1) | collective-permute-done | bytes 65568 | tf_op jit(solution)/shard_map/ppermute | solution.py:247
  149.7 18.2 %collective-permute-done.3 = f32[64,256]{1,0:T(8,128)S(1)} collective-permute-done((f32[64,256]{1,0:T(8,128)}, f32[64,256]{1,0:T(8,128)S(1)}, u32[]{:S(2)}, u32[]{:S(2)}) %collective-permute-start.3) | collective-permute-done | bytes 65568 | tf_op jit(solution)/shard_map/ppermute | solution.py:247
  167.9 0.9 dynamic-slice_dynamic-update-slice_fusion
  169.9 1.4 multiply_subtract_fusion.1
  171.2 2.9 %multiply_subtract_fusion.2 = (f32[64,2048]{1,0:T(8,128)}, f32[64,2048]{1,0:T(8,128)}, f32[64,2048]{1,0:T(8,128)}) fusion(f32[64,2048]{1,0:T(8,128)} %param.26, f32[64,2048]{1,0:T(8,128)} %reduce-scatter.2.cloned.1.call-done, f32[64,2048]{1,0:T(8,128)} %param.28, f32[64,2048]{1,0:T(8,128)} %param.27), kind=kLoop, calls=%fused_computation.25 | loop fusion | flops 1703936 | bytes 3670016 | tf_op jit(solution)/shard_map/sub | solution.py:38
  174.1 39.7 %all-gather.2.cloned.1.call-done = bf16[2048,2048]{1,0:T(8,128)(2,1)} async-done(((bf16[256,2048]{1,0:T(8,128)(2,1)}), bf16[2048,2048]{1,0:T(8,128)(2,1)}) %all-gather.2.cloned.1.call-update) | async-done | bytes 8388624 | tf_op jit(solution)/shard_map/all_gather | solution.py:190
  213.8 11.5 %multiply_subtract_fusion = (f32[1,256,2048]{2,1,0:T(8,128)}, f32[1,256,2048]{2,1,0:T(8,128)}, f32[1,256,2048]{2,1,0:T(8,128)}) fusion(f32[1,256,2048]{2,1,0:T(8,128)} %param.23, f32[1,256,2048]{2,1,0:T(8,128)} %param.25, f32[1,256,2048]{2,1,0:T(8,128)} %param.24, bf16[2048,256]{1,0:T(8,128)(2,1)S(1)} %bitcast.107, ...), kind=kOutput, calls=%fused_computation.11 | convolution fusion | flops 2154299392 | bytes 22020096 | tf_op jit(solution)/shard_map/dot_general | solution.py:26
  (69 shorter events, 10.1 us)
Async XLA Ops:
  7.2 40.8 %copy-start = (bf16[512,2048]{1,0:T(8,128)(2,1)S(1)}, bf16[512,2048]{1,0:T(8,128)(2,1)}, u32[]{:S(2)}) copy-start(bf16[512,2048]{1,0:T(8,128)(2,1)} %param.22) | copy-start | bytes 6291460
  7.2 164.0 %reduce-scatter.2.cloned.1.call-start = ((), (), s32[]{:S(2)}) async-start(), calls=%async_computation.2 | async-start | bytes 4718592 | tf_op jit(solution)/shard_map/reduce_scatter | solution.py:230
  7.2 6.6 %copy-start.7 = (f32[2048]{0:T(1024)S(1)}, f32[2048]{0:T(1024)}, u32[]{:S(2)}) copy-start(f32[2048]{0:T(1024)} %param.20) | copy-start | bytes 24580
  48.0 13.4 %copy-start.8 = (s32[4,64]{1,0:T(4,128)S(1)}, s32[4,64]{1,0:T(4,128)}, u32[]{:S(2)}) copy-start(s32[4,64]{1,0:T(4,128)} %param.19) | copy-start | bytes 3076
  48.0 13.4 %copy-start.1 = (bf16[256,2048]{1,0:T(8,128)(2,1)S(1)}, bf16[256,2048]{1,0:T(8,128)(2,1)}, u32[]{:S(2)}) copy-start(bf16[256,2048]{1,0:T(8,128)(2,1)} %spread.1) | copy-start | bytes 3145732
  50.1 0.8 copy-start.2
  65.4 148.4 %all-gather.2.cloned.1.call-start = ((), (), s32[]{:S(2)}) async-start(), calls=%async_computation.1 | async-start | bytes 9437184 | tf_op jit(solution)/shard_map/all_gather | solution.py:190
  97.0 3.7 %copy-start.9 = (s32[4,64]{1,0:T(4,128)S(1)}, s32[4,64]{1,0:T(4,128)}, u32[]{:S(2)}) copy-start(s32[4,64]{1,0:T(4,128)} %param.18) | copy-start | bytes 3076
  115.9 17.6 %copy-start.10 = (s32[8,1,256]{2,1,0:T(1,128)S(1)}, s32[8,1,256]{2,1,0:T(1,128)}, u32[]{:S(2)}) copy-start(s32[8,1,256]{2,1,0:T(1,128)} %get-tuple-element.12) | copy-start | bytes 24580
  134.3 0.8 copy-start.3
  135.8 8.3 %collective-permute-start = (f32[64,256]{1,0:T(8,128)}, f32[64,256]{1,0:T(8,128)S(1)}, u32[]{:S(2)}, u32[]{:S(2)}) collective-permute-start(f32[64,256]{1,0:T(8,128)} %get-tuple-element.28), channel_id=1, source_target_pairs={{0,7},{1,0},{2,1},{3,2},{4,3},{5,4},{6,5},{7,6},{8,15},{9,8},{10,9... | collective-permute-start | bytes 196616 | tf_op jit(solution)/shard_map/ppermute | solution.py:247
  139.9 9.5 %collective-permute-start.1 = (f32[64,256]{1,0:T(8,128)}, f32[64,256]{1,0:T(8,128)S(1)}, u32[]{:S(2)}, u32[]{:S(2)}) collective-permute-start(f32[64,256]{1,0:T(8,128)} %get-tuple-element.27), channel_id=1, source_target_pairs={{0,6},{1,7},{2,0},{3,1},{4,2},{5,3},{6,4},{7,5},{8,14},{9,15},{10,... | collective-permute-start | bytes 196616 | tf_op jit(solution)/shard_map/ppermute | solution.py:247
  139.9 9.8 %collective-permute-start.2 = (f32[64,256]{1,0:T(8,128)}, f32[64,256]{1,0:T(8,128)S(1)}, u32[]{:S(2)}, u32[]{:S(2)}) collective-permute-start(f32[64,256]{1,0:T(8,128)} %get-tuple-element.26), channel_id=1, source_target_pairs={{0,5},{1,6},{2,7},{3,0},{4,1},{5,2},{6,3},{7,4},{8,13},{9,14},{10,... | collective-permute-start | bytes 196616 | tf_op jit(solution)/shard_map/ppermute | solution.py:247
  140.3 27.5 %collective-permute-start.3 = (f32[64,256]{1,0:T(8,128)}, f32[64,256]{1,0:T(8,128)S(1)}, u32[]{:S(2)}, u32[]{:S(2)}) collective-permute-start(f32[64,256]{1,0:T(8,128)} %get-tuple-element.25), channel_id=1, source_target_pairs={{0,4},{1,5},{2,6},{3,7},{4,0},{5,1},{6,2},{7,3},{8,12},{9,13},{10,... | collective-permute-start | bytes 196616 | tf_op jit(solution)/shard_map/ppermute | solution.py:247
  142.5 25.3 %collective-permute-start.4 = (f32[64,256]{1,0:T(8,128)}, f32[64,256]{1,0:T(8,128)S(1)}, u32[]{:S(2)}, u32[]{:S(2)}) collective-permute-start(f32[64,256]{1,0:T(8,128)} %get-tuple-element.24), channel_id=1, source_target_pairs={{0,3},{1,4},{2,5},{3,6},{4,7},{5,0},{6,1},{7,2},{8,11},{9,12},{10,... | collective-permute-start | bytes 196616 | tf_op jit(solution)/shard_map/ppermute | solution.py:247
  144.1 25.8 %copy-start.4 = (f32[64,2048]{1,0:T(8,128)S(1)}, f32[64,2048]{1,0:T(8,128)}, u32[]{:S(2)}) copy-start(f32[64,2048]{1,0:T(8,128)} %param.29) | copy-start | bytes 1572868
  144.1 25.8 %copy-start.5 = (f32[64,2048]{1,0:T(8,128)S(1)}, f32[64,2048]{1,0:T(8,128)}, u32[]{:S(2)}) copy-start(f32[64,2048]{1,0:T(8,128)} %param.31) | copy-start | bytes 1572868
  144.1 25.8 %copy-start.6 = (f32[64,2048]{1,0:T(8,128)S(1)}, f32[64,2048]{1,0:T(8,128)}, u32[]{:S(2)}) copy-start(f32[64,2048]{1,0:T(8,128)} %param.30) | copy-start | bytes 1572868
  144.1 23.8 %collective-permute-start.5 = (f32[64,256]{1,0:T(8,128)}, f32[64,256]{1,0:T(8,128)S(1)}, u32[]{:S(2)}, u32[]{:S(2)}) collective-permute-start(f32[64,256]{1,0:T(8,128)} %get-tuple-element.23), channel_id=1, source_target_pairs={{0,2},{1,3},{2,4},{3,5},{4,6},{5,7},{6,0},{7,1},{8,10},{9,11},{10,... | collective-permute-start | bytes 196616 | tf_op jit(solution)/shard_map/ppermute | solution.py:247
  149.4 18.6 %collective-permute-start.6 = (f32[64,256]{1,0:T(8,128)S(1)}, f32[64,256]{1,0:T(8,128)S(1)}, u32[]{:S(2)}, u32[]{:S(2)}) collective-permute-start(f32[64,256]{1,0:T(8,128)S(1)} %get-tuple-element.22), channel_id=1, source_target_pairs={{0,1},{1,2},{2,3},{3,4},{4,5},{5,6},{6,7},{7,0},{8,9},{9,10},{10,1... | collective-permute-start | bytes 196616 | tf_op jit(solution)/shard_map/ppermute | solution.py:247
Sparse Core Ops, SparseCore 0:
  65.5 54.5 reduce-scatter.1
  121.6 92.1 all-gather.1
